TPU v7x, 32 devices: a whole 2x2x4 slice. The times are simulated.
32 devices in a mesh: ba: 4 (over x, core), ma: 4 (over z), row: 2 (over y).
Axes of the slice: x: 2, y: 2, z: 4, core: 2. Of those that a mesh axis runs over, the one named last changes fastest.
Arguments:
- tokens: bfloat16 [8, 256, 4096], P(('ba', 'row'), None, 'ma'), may hold values from -6 to 6
- attn_gain: bfloat16 [4096], P('ma'), may hold values from 0.25 to 1.75
- query_weight: bfloat16 [4096, 4096], P('row', 'ma'), may hold values from -0.046875 to 0.046875
- key_weight: bfloat16 [4096, 4096], P('row', 'ma'), may hold values from -0.046875 to 0.046875
- value_projection_matrix: bfloat16 [4096, 4096], P('row', 'ma'), may hold values from -0.09375 to 0.09375
- attention_output_matrix: bfloat16 [4096, 4096], P('ma', 'row'), may hold values from -0.125 to 0.125
- bucket_bias_matrix: float32 [32, 64], P(None, 'ma'), may hold values from -6 to 215, as said below
- ffn_gain: bfloat16 [4096], P('ma'), may hold values from 0.25 to 1.75
- gate_weight: bfloat16 [4096, 8192], P(None, ('ma', 'row')), may hold values from -0.09375 to 0.09375
- up_weight: bfloat16 [4096, 8192], P(None, ('ma', 'row')), may hold values from -0.09375 to 0.09375
- down_projection_weight: bfloat16 [8192, 4096], P(('ma', 'row')), may hold values from -0.09375 to 0.09375
Outputs:
- encoded: bfloat16 [8, 256, 4096], P(('ba', 'row'), None, 'ma')
Inputs may be any that keep to these rules, and one draw needn't show every extreme that they name: `bucket_bias_matrix`: entries of the relative position table.
All inputs are finite; a program needn't handle non-finite values.
Results may differ from a plain program's by a relative error of at most 0.017.
Values may be sent and summed in bfloat16 or wider, within the bound.
A program may use at most 128 MiB of HBM per device.

v0:
```python
import jax
import jax.numpy as jnp
from jax import lax
from jax.sharding import PartitionSpec as P

bucket_thresholds = (1, 2, 3, 4, 5, 6, 7, 8, 11, 16, 23, 32, 45, 64, 91, 128)
epsilon = 1e-06


def buckets(length):
    places = jnp.arange(length, dtype=jnp.int32)
    offset = places[None, :] - places[:, None]
    distance = jnp.abs(offset)
    backward = jnp.zeros_like(distance)
    for threshold in bucket_thresholds[:15]:
        backward = backward + (distance >= threshold).astype(jnp.int32)
    forward = jnp.full_like(distance, 15)
    for threshold in bucket_thresholds:
        forward = forward + (distance >= threshold).astype(jnp.int32)
    return jnp.where(offset > 0, forward, backward)


def rms_scale(values, gain):
    mean_square = jnp.mean(values * values, axis=-1, keepdims=True)
    return (values * lax.rsqrt(mean_square + epsilon) * gain.astype(jnp.float32)).astype(
        jnp.bfloat16
    )


def regroup(values, norm_gain_vector):
    widened = (
        lax.all_gather(values, "ma", axis=1, tiled=True),
        lax.all_gather(norm_gain_vector, "ma", axis=1, tiled=True),
    )
    stacked = lax.all_gather(widened[0], "row", axis=0, tiled=True)
    return (stacked, widened[1])


def on_device(
    tokens,
    attn_gain,
    query_weight,
    key_weight,
    value_projection_matrix,
    attention_output_matrix,
    bucket_bias_matrix,
    ffn_gain,
    gate_weight,
    up_weight,
    down_projection_weight,
):
    sequences, length, part_width = tokens.shape
    ma_count = lax.axis_size("ma")
    local_heads = bucket_bias_matrix.shape[1]
    inner_width = query_weight.shape[1]
    head_size = inner_width // local_heads
    slab_rows = sequences * length
    token_rows = tokens.reshape(slab_rows, part_width)
    token_float = token_rows.astype(jnp.float32)
    full_weights = (
        lax.all_gather(query_weight, "row", axis=0, tiled=True),
        lax.all_gather(key_weight, "row", axis=0, tiled=True),
        lax.all_gather(value_projection_matrix, "row", axis=0, tiled=True),
    )
    whole_rows, whole_gain = (
        lax.all_gather(token_rows, "ma", axis=1, tiled=True),
        lax.all_gather(attn_gain.reshape(1, part_width), "ma", axis=1, tiled=True),
    )
    normed = rms_scale(whole_rows.astype(jnp.float32), whole_gain[0])
    projected = tuple(
        (jnp.dot(normed, matrix, preferred_element_type=jnp.float32) for matrix in full_weights)
    )
    query_heads, key_heads, value_heads = [
        member.astype(jnp.bfloat16).reshape(sequences, length, local_heads, head_size)
        for member in projected
    ]
    bucket_grid = buckets(length)
    table_rows = jnp.arange(bucket_bias_matrix.shape[0], dtype=jnp.int32)
    bucket_indicator = (table_rows[:, None, None] == bucket_grid[None, :, :]).astype(jnp.float32)
    relative_position_scores = jnp.einsum(
        "dmy,du->umy", bucket_indicator, bucket_bias_matrix, precision=lax.Precision.HIGHEST
    )
    scores = (
        jnp.einsum("sqhd,skhd->shqk", query_heads, key_heads, preferred_element_type=jnp.float32)
        + relative_position_scores[None]
    )
    row_max = jnp.max(scores, axis=-1, keepdims=True)
    exponent = jnp.exp(scores - row_max)
    weights = (exponent / jnp.sum(exponent, axis=-1, keepdims=True)).astype(jnp.bfloat16)
    attended = jnp.einsum(
        "shqk,skhd->sqhd", weights, value_heads, preferred_element_type=jnp.float32
    )
    attended = attended.astype(jnp.bfloat16).reshape(slab_rows, inner_width)
    partial_out = jnp.dot(
        attended,
        lax.all_gather(attention_output_matrix, "row", axis=1, tiled=True),
        preferred_element_type=jnp.float32,
    )
    attn_out = lax.psum_scatter(
        partial_out.astype(jnp.bfloat16), "ma", scatter_dimension=1, tiled=True
    ).astype(jnp.float32)
    residual_stream = (token_float + attn_out).astype(jnp.bfloat16)
    residual_f = residual_stream.astype(jnp.float32)
    norm_gain_vector = ffn_gain.reshape(1, part_width)
    gate_full, up_full, down_full = (gate_weight, up_weight, down_projection_weight)
    group_rows, group_gain = regroup(residual_stream, norm_gain_vector)
    ffn_in = rms_scale(group_rows.astype(jnp.float32), group_gain[0])
    gate_act = jnp.dot(ffn_in, gate_full, preferred_element_type=jnp.float32)
    up_act = jnp.dot(ffn_in, up_full, preferred_element_type=jnp.float32)
    hidden = (jax.nn.gelu(gate_act, approximate=True) * up_act).astype(jnp.bfloat16)
    down_blocks = down_full.reshape(down_full.shape[0], ma_count, part_width)
    down_terms = jnp.einsum("tf,fmd->mtd", hidden, down_blocks, preferred_element_type=jnp.float32)
    down_terms = down_terms.reshape(ma_count * ffn_in.shape[0], part_width)
    ffn_out = lax.psum_scatter(
        down_terms.astype(jnp.bfloat16), ("ma", "row"), scatter_dimension=0, tiled=True
    ).astype(jnp.float32)
    encoded = (residual_f + ffn_out).astype(jnp.bfloat16)
    return encoded.reshape(sequences, length, part_width)


def solution(mesh):
    in_specs = (
        P(("ba", "row"), None, "ma"),
        P("ma"),
        P("row", "ma"),
        P("row", "ma"),
        P("row", "ma"),
        P("ma", "row"),
        P(None, "ma"),
        P("ma"),
        P(None, ("ma", "row")),
        P(None, ("ma", "row")),
        P(("ma", "row"), None),
    )
    out_specs = P(("ba", "row"), None, "ma")
    return jax.shard_map(
        on_device, mesh=mesh, in_specs=in_specs, out_specs=out_specs, check_vma=False
    )
```

profile of v0, /device:TPU:0, one launch (start us, length us, event | category | flops | bytes accessed | tf_op | source)
XLA Modules:
  0.0 752.7 jit_solution(16300057747724244085)
XLA Ops:
  6.5 0.0 copy-start
  6.5 0.0 all-gather.23.cloned.1.call-start
  6.5 0.7 all-gather.23.cloned.1.call-update
  7.3 0.0 all-gather.13.cloned.1.call-start
  7.3 0.7 all-gather.13.cloned.1.call-update
  8.0 0.0 all-gather.15.cloned.1.call-start
  8.1 0.7 all-gather.15.cloned.1.call-update
  8.7 0.0 copy-start.7
  8.8 0.0 all-gather.11.cloned.1.call-start
  8.8 0.5 all-gather.11.cloned.1.call-update
  9.3 0.0 all-gather.17.cloned.1.call-start
  9.4 0.5 all-gather.17.cloned.1.call-update
  9.9 0.0 reduce-scatter.3.cloned.1.call-start
  10.0 0.0 copy-done.7
  10.0 13.7 %all-gather.1 = bf16[4096]{0:T(1024)(128)(2,1)S(1)} all-gather(bf16[1024]{0:T(1024)(128)(2,1)S(1)} %copy-done.7), channel_id=3, replica_groups=mesh['ba'=4,'ma'=4,'row'=2] {'ma'}, dimensions={0}, use_global_device_ids=true | all-gather | bytes 10240 | tf_op jit(solution)/shard_map/all_gather | solution.py:67
  23.7 0.3 fusion.33
  24.1 0.0 copy-done
  24.1 4.2 fusion.7
  28.3 5.3 copy.27
  33.6 23.8 %all-gather.23.cloned.1.call-done = bf16[1,256,4096]{2,1,0:T(8,128)(2,1)} async-done(((bf16[1,256,1024]{2,1,0:T(8,128)(2,1)}), bf16[1,256,4096]{2,1,0:T(8,128)(2,1)}) %all-gather.23.cloned.1.call-update) | async-done | bytes 2097168 | tf_op jit(solution)/shard_map/all_gather | solution.py:66
  57.3 2.1 fusion.8
  59.4 102.2 %all-gather.13.cloned.1.call-done = bf16[4096,1024]{1,0:T(8,128)(2,1)} async-done(((bf16[2048,1024]{1,0:T(8,128)(2,1)}), bf16[4096,1024]{1,0:T(8,128)(2,1)}) %all-gather.13.cloned.1.call-update) | async-done | bytes 8388624 | tf_op jit(solution)/shard_map/all_gather | solution.py:61
  161.7 6.4 convolution_convert_fusion.2
  168.1 0.2 copy.25
  168.3 99.0 %all-gather.15.cloned.1.call-done = bf16[4096,1024]{1,0:T(8,128)(2,1)} async-done(((bf16[2048,1024]{1,0:T(8,128)(2,1)}), bf16[4096,1024]{1,0:T(8,128)(2,1)}) %all-gather.15.cloned.1.call-update) | async-done | bytes 8388624 | tf_op jit(solution)/shard_map/all_gather | solution.py:62
  267.3 0.0 copy-done.6
  267.3 6.6 convolution_convert_fusion.1
  273.9 1.3 copy.26
  275.2 97.5 %all-gather.11.cloned.1.call-done = bf16[4096,1024]{1,0:T(8,128)(2,1)} async-done(((bf16[2048,1024]{1,0:T(8,128)(2,1)}), bf16[4096,1024]{1,0:T(8,128)(2,1)}) %all-gather.11.cloned.1.call-update) | async-done | bytes 8388624 | tf_op jit(solution)/shard_map/all_gather | solution.py:63
  372.7 6.6 convolution_convert_fusion.3
  379.3 1.3 copy.24
  380.6 3.6 bitcast_add_fusion
  384.3 0.0 copy-start.2
  384.3 2.0 copy-done.2
  386.3 0.8 fusion.57
  387.1 5.3 fusion.26
  392.3 85.8 %all-gather.17.cloned.1.call-done = bf16[1024,4096]{1,0:T(8,128)(2,1)} async-done(((bf16[1024,2048]{1,0:T(8,128)(2,1)}), bf16[1024,4096]{1,0:T(8,128)(2,1)}) %all-gather.17.cloned.1.call-update) | async-done | bytes 8388624 | tf_op jit(solution)/shard_map/all_gather | solution.py:96
  478.1 7.2 convolution_convert_fusion
  485.3 0.0 reduce-scatter.3.cloned.1.call-update
  485.4 0.0 all-gather.19.cloned.1.call-start
  485.4 43.7 %reduce-scatter.3.cloned.1.call-done = bf16[256,1024]{1,0:T(8,128)(2,1)} async-done(((bf16[256,4096]{1,0:T(8,128)(2,1)}), bf16[256,1024]{1,0:T(8,128)(2,1)}) %reduce-scatter.3.cloned.1.call-update) | async-done | bytes 524304 | tf_op jit(solution)/shard_map/reduce_scatter | solution.py:99
  529.1 0.0 copy-done.5
  529.1 2.0 fusion.30
  531.2 0.0 all-gather.19.cloned.1.call-update
  531.2 0.0 all-gather.21.cloned.1.call-start
  531.2 45.0 %all-gather.19.cloned.1.call-done = bf16[256,4096]{1,0:T(8,128)(2,1)} async-done(((bf16[256,1024]{1,0:T(8,128)(2,1)}), bf16[256,4096]{1,0:T(8,128)(2,1)}) %all-gather.19.cloned.1.call-update) | async-done | bytes 2097168 | tf_op jit(solution)/shard_map/all_gather | solution.py:32
  576.2 0.0 all-gather.21.cloned.1.call-update
  576.2 0.0 reduce-scatter.5.cloned.1.call-start
  576.3 0.0 copy-done.8
  576.3 12.2 %all-gather.2 = bf16[4096]{0:T(1024)(128)(2,1)S(1)} all-gather(bf16[1024]{0:T(1024)(128)(2,1)S(1)} %copy-done.8), channel_id=4, replica_groups=mesh['ba'=4,'ma'=4,'row'=2] {'ma'}, dimensions={0}, use_global_device_ids=true | all-gather | bytes 10240 | tf_op jit(solution)/shard_map/all_gather | solution.py:33
  588.5 44.9 %all-gather.21.cloned.1.call-done = bf16[512,4096]{1,0:T(8,128)(2,1)} async-done(((bf16[256,4096]{1,0:T(8,128)(2,1)}), bf16[512,4096]{1,0:T(8,128)(2,1)}) %all-gather.21.cloned.1.call-update) | async-done | bytes 4194320 | tf_op jit(solution)/shard_map/all_gather | solution.py:35
  633.3 3.2 fusion.1
  636.6 0.2 copy-done.4
  636.8 7.7 %fusion.28 = f32[512,1024]{1,0:T(8,128)S(1)} fusion(bf16[4096,1024]{1,0:T(8,128)(2,1)} %param.19, bf16[512,4096]{1,0:T(8,128)(2,1)S(1)} %copy-done.4, f32[4096]{0:T(1024)S(1)} %mul.97, f32[512]{0:T(512)S(1)} %add_rsqrt_fusion), kind=kOutput, calls=%fused_computation.38 | convolution fusion | flops 4303355904 | bytes 14698496 | tf_op jit(solution)/shard_map/dot_general | solution.py:108
  644.5 0.0 slice-done
  644.5 0.0 slice-done.1
  644.6 4.9 fusion.25
  649.4 0.0 slice-done.2
  649.4 0.0 slice-done.3
  649.5 0.0 copy-start.1
  649.5 6.2 fusion.12
  655.6 0.0 reduce-scatter.5.cloned.1.call-update
  655.6 88.5 %reduce-scatter.5.cloned.1.call-done = bf16[256,1024]{1,0:T(8,128)(2,1)} async-done(((bf16[2048,1024]{1,0:T(8,128)(2,1)}), bf16[256,1024]{1,0:T(8,128)(2,1)}) %reduce-scatter.5.cloned.1.call-update) | async-done | bytes 524304 | tf_op jit(solution)/shard_map/reduce_scatter | solution.py:114
  744.1 2.0 fusion.31
  (17 shorter events, 0.0 us)
Async XLA Ops:
  6.5 17.5 %copy-start = (f32[32,16]{0,1:T(8,128)S(1)}, f32[32,16]{0,1:T(8,128)}, u32[]{:S(2)}) copy-start(f32[32,16]{0,1:T(8,128)} %param.17) | copy-start | bytes 6148
  6.5 50.8 %all-gather.23.cloned.1.call-start = ((), (), s32[]{:S(2)}) async-start(), calls=%async_computation.10 | async-start | bytes 2621440 | tf_op jit(solution)/shard_map/all_gather | solution.py:66
  7.3 154.4 %all-gather.13.cloned.1.call-start = ((), (), s32[]{:S(2)}) async-start(), calls=%async_computation.3 | async-start | bytes 12582912 | tf_op jit(solution)/shard_map/all_gather | solution.py:61
  8.0 259.3 %all-gather.15.cloned.1.call-start = ((), (), s32[]{:S(2)}) async-start(), calls=%async_computation.4 | async-start | bytes 12582912 | tf_op jit(solution)/shard_map/all_gather | solution.py:62
  8.7 1.2 copy-start.7
  8.8 363.9 %all-gather.11.cloned.1.call-start = ((), (), s32[]{:S(2)}) async-start(), calls=%async_computation.2 | async-start | bytes 12582912 | tf_op jit(solution)/shard_map/all_gather | solution.py:63
  9.3 468.8 %all-gather.17.cloned.1.call-start = ((), (), s32[]{:S(2)}) async-start(), calls=%async_computation.5 | async-start | bytes 12582912 | tf_op jit(solution)/shard_map/all_gather | solution.py:96
  9.9 519.2 %reduce-scatter.3.cloned.1.call-start = ((), (), s32[]{:S(2)}) async-start(), calls=%async_computation.6 | async-start | bytes 2621440 | tf_op jit(solution)/shard_map/reduce_scatter | solution.py:99
  59.4 207.9 %copy-start.6 = (bf16[1,256,4096]{2,1,0:T(8,128)(2,1)S(1)}, bf16[1,256,4096]{2,1,0:T(8,128)(2,1)}, u32[]{:S(2)}) copy-start(bf16[1,256,4096]{2,1,0:T(8,128)(2,1)} %all-gather.23.cloned.1.call-done) | copy-start | bytes 6291460
  384.3 2.1 copy-start.2
  478.1 51.0 %copy-start.5 = (bf16[1,256,1024]{2,1,0:T(8,128)(2,1)S(1)}, bf16[1,256,1024]{2,1,0:T(8,128)(2,1)}, u32[]{:S(2)}) copy-start(bf16[1,256,1024]{2,1,0:T(8,128)(2,1)} %param.11) | copy-start | bytes 1572868
  485.3 91.0 %copy-start.8 = (bf16[1024]{0:T(1024)(128)(2,1)S(1)}, bf16[1024]{0:T(1024)(128)(2,1)}, u32[]{:S(2)}) copy-start(bf16[1024]{0:T(1024)(128)(2,1)} %param.18) | copy-start | bytes 6148
  485.4 90.9 %all-gather.19.cloned.1.call-start = ((), (), s32[]{:S(2)}) async-start(), calls=%async_computation.7 | async-start | bytes 2621440 | tf_op jit(solution)/shard_map/all_gather | solution.py:32
  531.2 102.1 %all-gather.21.cloned.1.call-start = ((), (), s32[]{:S(2)}) async-start(), calls=%async_computation.8 | async-start | bytes 6291456 | tf_op jit(solution)/shard_map/all_gather | solution.py:35
  576.2 167.9 %reduce-scatter.5.cloned.1.call-start = ((), (), s32[]{:S(2)}) async-start(), calls=%async_computation.9 | async-start | bytes 4718592 | tf_op jit(solution)/shard_map/reduce_scatter | solution.py:114
  633.3 3.4 copy-start.4
  633.3 11.2 %slice-start = ((s8[8388608]{0:T(1024)(128)(4,1)}), s8[4194304]{0:T(1024)(128)(4,1)S(1)}, s32[]{:S(2)}) async-start(s8[8388608]{0:T(1024)(128)(4,1)} %bitcast.54), calls=%async_computation.11 | async-start | bytes 8388608
  633.3 16.1 %slice-start.2 = ((s8[8388608]{0:T(1024)(128)(4,1)}), s8[4194304]{0:T(1024)(128)(4,1)S(1)}, s32[]{:S(2)}) async-start(s8[8388608]{0:T(1024)(128)(4,1)} %bitcast.56), calls=%async_computation.13 | async-start | bytes 8388608
  636.8 7.8 %slice-start.1 = ((s8[8388608]{0:T(1024)(128)(4,1)}), s8[4194304]{0:T(1024)(128)(4,1)S(1)}, s32[]{:S(2)}) async-start(s8[8388608]{0:T(1024)(128)(4,1)} %bitcast.54), calls=%async_computation.12 | async-start | bytes 8388608
  636.8 12.7 %slice-start.3 = ((s8[8388608]{0:T(1024)(128)(4,1)}), s8[4194304]{0:T(1024)(128)(4,1)S(1)}, s32[]{:S(2)}) async-start(s8[8388608]{0:T(1024)(128)(4,1)} %bitcast.56), calls=%async_computation.14 | async-start | bytes 8388608
  649.5 96.7 %copy-start.1 = (f32[32,16]{0,1:T(8,128)S(1)}, f32[32,16]{0,1:T(8,128)}, u32[]{:S(2)}) copy-start(f32[32,16]{0,1:T(8,128)} %param.17) | copy-start | bytes 6148
  655.6 88.5 %copy-start.3 = (bf16[256,1024]{1,0:T(8,128)(2,1)S(1)}, bf16[256,1024]{1,0:T(8,128)(2,1)}, u32[]{:S(2)}) copy-start(bf16[256,1024]{1,0:T(8,128)(2,1)} %fusion.30) | copy-start | bytes 1572868
Sparse Core Ops, SparseCore 0:
  8.9 48.3 all-gather.22
  58.9 102.7 all-gather.12
  163.2 104.0 all-gather.14
  268.7 103.9 all-gather.10
  374.1 103.9 all-gather.16
  485.5 43.6 reduce-scatter.2
  531.3 44.8 all-gather.18
  577.8 55.5 all-gather.20
  655.8 88.3 reduce-scatter.4
where the time goes:
time: 753 us
  waiting for transfers between devices  634 us (84%)
  matrix products  58.6 us (8%)
  blocking collectives  25.9 us (3%)
  between operations  13.4 us (2%)
  other arithmetic  10.5 us (1%)
  local copies, waits for them, and re-layouts  10.4 us (1%)
    all_gather x1, waiting for transfers between devices, on_device(): lax.all_gather(query_weight, 'row', axis=0, tiled=True)  102 us
    all_gather x1, waiting for transfers between devices, on_device(): lax.all_gather(key_weight, 'row', axis=0, tiled=True)  99 us
    all_gather x1, waiting for transfers between devices, on_device(): lax.all_gather(value_projection_matrix, 'row', axis=0, tiled=True)  97.5 us
    reduce_scatter x1, waiting for transfers between devices, on_device(): lax.psum_scatter(down_terms.astype(jnp.bfloat16), ('ma', 'row'), scatter_...  88.5 us
    all_gather x1, waiting for transfers between devices, on_device(): lax.all_gather(attention_output_matrix, 'row', axis=1, tiled=True)  85.8 us
    all_gather x1, waiting for transfers between devices, regroup(): lax.all_gather(values, 'ma', axis=1, tiled=True)  45 us
    all_gather x1, waiting for transfers between devices, regroup(): stacked = lax.all_gather(widened[0], 'row', axis=0, tiled=True)  44.9 us
    reduce_scatter x1, waiting for transfers between devices, on_device(): lax.psum_scatter(partial_out.astype(jnp.bfloat16), 'ma', scatter_dimensio...  43.7 us
  transfers between devices with their start and end apart: 9, of which 9 were waited for; matrix products, arithmetic and copies ran while one was open for 6% of the time, Pallas kernels for 0%

commit v1 on v0

--- a/solution.py
+++ b/solution.py
@@ -5,6 +5,19 @@
 
 bucket_thresholds = (1, 2, 3, 4, 5, 6, 7, 8, 11, 16, 23, 32, 45, 64, 91, 128)
 epsilon = 1e-06
+
+
+def gather_around(shard, axis, dim):
+    length, mine, span = (lax.axis_size(axis), lax.axis_index(axis), shard.shape[dim])
+    right = [(i, (i + 1) % length) for i in range(length)]
+    out = jnp.zeros((*shard.shape[:dim], length * span, *shard.shape[dim + 1 :]), shard.dtype)
+    block = shard
+    for step in range(length):
+        source = (mine - step) % length
+        out = lax.dynamic_update_slice_in_dim(out, block, source * span, axis=dim)
+        if step < length - 1:
+            block = lax.ppermute(block, axis, right)
+    return out
 
 
 def buckets(length):
@@ -29,7 +42,7 @@
 
 def regroup(values, norm_gain_vector):
     widened = (
-        lax.all_gather(values, "ma", axis=1, tiled=True),
+        gather_around(values, "ma", 1),
         lax.all_gather(norm_gain_vector, "ma", axis=1, tiled=True),
     )
     stacked = lax.all_gather(widened[0], "row", axis=0, tiled=True)

time: 753 us -> 752 us (level)
    all_gather x1 -> x0, waiting for transfers between devices: 45 us -> none  [regroup(): lax.all_gather(values, 'ma', axis=1, tiled=True)]
    ppermute x0 -> x3, waiting for transfers between devices: none -> 41.2 us  [gather_around(): block = lax.ppermute(block, axis, right)]
  transfers between devices with their start and end apart: 9 -> 11, of which waited for: 9 -> 11; matrix products, arithmetic and copies ran while one was open for 6% -> 6% of each run, Pallas kernels for 0% -> 0%
where the time goes in v1:
time: 752 us; the launch traced here: 751 us
  waiting for transfers between devices  628 us (84%)
  matrix products  58.6 us (8%)
  blocking collectives  25.9 us (3%)
  local copies, waits for them, and re-layouts  14.3 us (2%)
  between operations  13.7 us (2%)
  other arithmetic  9.75 us (1%)
    all_gather x1, waiting for transfers between devices, on_device(): lax.all_gather(query_weight, 'row', axis=0, tiled=True)  102 us
    all_gather x1, waiting for transfers between devices, on_device(): lax.all_gather(key_weight, 'row', axis=0, tiled=True)  99 us
    all_gather x1, waiting for transfers between devices, on_device(): lax.all_gather(value_projection_matrix, 'row', axis=0, tiled=True)  97.5 us
    reduce_scatter x1, waiting for transfers between devices, on_device(): lax.psum_scatter(down_terms.astype(jnp.bfloat16), ('ma', 'row'), scatter_...  88.5 us
    all_gather x1, waiting for transfers between devices, on_device(): lax.all_gather(attention_output_matrix, 'row', axis=1, tiled=True)  85.8 us
    reduce_scatter x1, waiting for transfers between devices, on_device(): lax.psum_scatter(partial_out.astype(jnp.bfloat16), 'ma', scatter_dimensio...  43.7 us
    all_gather x1, waiting for transfers between devices, regroup(): stacked = lax.all_gather(widened[0], 'row', axis=0, tiled=True)  42.8 us
    ppermute x3, waiting for transfers between devices, gather_around(): block = lax.ppermute(block, axis, right)  41.2 us
  transfers between devices with their start and end apart: 11, of which 11 were waited for; matrix products, arithmetic and copies ran while one was open for 6% of the time, Pallas kernels for 0%

profile of v1, /device:TPU:0, one launch (start us, length us, event | category | flops | bytes accessed | tf_op | source)
XLA Modules:
  0.0 750.9 jit_solution(8895643880934201229)
XLA Ops:
  6.5 0.0 all-gather.20.cloned.1.call-start
  6.5 0.7 all-gather.20.cloned.1.call-update
  7.3 0.0 all-gather.12.cloned.1.call-start
  7.3 0.7 all-gather.12.cloned.1.call-update
  8.0 0.0 all-gather.14.cloned.1.call-start
  8.1 0.7 all-gather.14.cloned.1.call-update
  8.8 0.0 all-gather.10.cloned.1.call-start
  8.8 0.5 all-gather.10.cloned.1.call-update
  9.3 0.0 all-gather.16.cloned.1.call-start
  9.4 0.5 all-gather.16.cloned.1.call-update
  9.9 0.0 reduce-scatter.3.cloned.1.call-start
  10.0 13.7 %all-gather.1 = bf16[4096]{0:T(1024)(128)(2,1)S(1)} all-gather(bf16[1024]{0:T(1024)(128)(2,1)S(1)} %copy-done.7), channel_id=3, replica_groups=mesh['ba'=4,'ma'=4,'row'=2] {'ma'}, dimensions={0}, use_global_device_ids=true | all-gather | bytes 10240 | tf_op jit(solution)/shard_map/all_gather | solution.py:80
  23.7 0.3 fusion.33
  24.1 4.2 fusion.7
  28.3 5.3 copy.27
  33.6 23.7 %all-gather.20.cloned.1.call-done = bf16[1,256,4096]{2,1,0:T(8,128)(2,1)} async-done(((bf16[1,256,1024]{2,1,0:T(8,128)(2,1)}), bf16[1,256,4096]{2,1,0:T(8,128)(2,1)}) %all-gather.20.cloned.1.call-update) | async-done | bytes 2097168 | tf_op jit(solution)/shard_map/all_gather | solution.py:79
  57.3 2.1 fusion.8
  59.4 102.2 %all-gather.12.cloned.1.call-done = bf16[4096,1024]{1,0:T(8,128)(2,1)} async-done(((bf16[2048,1024]{1,0:T(8,128)(2,1)}), bf16[4096,1024]{1,0:T(8,128)(2,1)}) %all-gather.12.cloned.1.call-update) | async-done | bytes 8388624 | tf_op jit(solution)/shard_map/all_gather | solution.py:74
  161.7 6.4 convolution_convert_fusion.2
  168.1 0.2 copy.25
  168.3 99.0 %all-gather.14.cloned.1.call-done = bf16[4096,1024]{1,0:T(8,128)(2,1)} async-done(((bf16[2048,1024]{1,0:T(8,128)(2,1)}), bf16[4096,1024]{1,0:T(8,128)(2,1)}) %all-gather.14.cloned.1.call-update) | async-done | bytes 8388624 | tf_op jit(solution)/shard_map/all_gather | solution.py:75
  267.3 6.6 convolution_convert_fusion.1
  273.9 1.3 copy.26
  275.2 97.5 %all-gather.10.cloned.1.call-done = bf16[4096,1024]{1,0:T(8,128)(2,1)} async-done(((bf16[2048,1024]{1,0:T(8,128)(2,1)}), bf16[4096,1024]{1,0:T(8,128)(2,1)}) %all-gather.10.cloned.1.call-update) | async-done | bytes 8388624 | tf_op jit(solution)/shard_map/all_gather | solution.py:76
  372.7 6.6 convolution_convert_fusion.3
  379.3 1.3 copy.24
  380.6 3.6 bitcast_add_fusion
  384.3 2.0 copy-done.2
  386.3 0.8 fusion.58
  387.1 5.3 fusion.26
  392.3 85.8 %all-gather.16.cloned.1.call-done = bf16[1024,4096]{1,0:T(8,128)(2,1)} async-done(((bf16[1024,2048]{1,0:T(8,128)(2,1)}), bf16[1024,4096]{1,0:T(8,128)(2,1)}) %all-gather.16.cloned.1.call-update) | async-done | bytes 8388624 | tf_op jit(solution)/shard_map/all_gather | solution.py:109
  478.1 7.2 convolution_convert_fusion
  485.3 0.0 reduce-scatter.3.cloned.1.call-update
  485.3 0.0 all-gather.18.cloned.1.call-start
  485.4 43.7 %reduce-scatter.3.cloned.1.call-done = bf16[256,1024]{1,0:T(8,128)(2,1)} async-done(((bf16[256,4096]{1,0:T(8,128)(2,1)}), bf16[256,1024]{1,0:T(8,128)(2,1)}) %reduce-scatter.3.cloned.1.call-update) | async-done | bytes 524304 | tf_op jit(solution)/shard_map/reduce_scatter | solution.py:112
  529.1 0.2 broadcast_in_dim.5
  529.3 0.0 copy-start.8
  529.3 1.3 constant_dynamic-update-slice_fusion.3
  530.6 0.7 collective-permute-start
  531.3 14.4 %collective-permute-done = bf16[256,1024]{1,0:T(8,128)(2,1)S(1)} collective-permute-done((bf16[256,1024]{1,0:T(8,128)(2,1)S(1)}, bf16[256,1024]{1,0:T(8,128)(2,1)S(1)}, u32[]{:S(2)}, u32[]{:S(2)}) %collective-permute-start) | collective-permute-done | bytes 524320 | tf_op jit(solution)/shard_map/ppermute | solution.py:19
  545.7 0.0 collective-permute-start.1
  545.7 14.3 %collective-permute-done.1 = bf16[256,1024]{1,0:T(8,128)(2,1)} collective-permute-done((bf16[256,1024]{1,0:T(8,128)(2,1)S(1)}, bf16[256,1024]{1,0:T(8,128)(2,1)}, u32[]{:S(2)}, u32[]{:S(2)}) %collective-permute-start.1) | collective-permute-done | bytes 524320 | tf_op jit(solution)/shard_map/ppermute | solution.py:19
  560.0 0.0 collective-permute-start.2
  560.1 1.1 constant_dynamic-update-slice_fusion.1
  561.2 12.5 %collective-permute-done.2 = bf16[256,1024]{1,0:T(8,128)(2,1)} collective-permute-done((bf16[256,1024]{1,0:T(8,128)(2,1)}, bf16[256,1024]{1,0:T(8,128)(2,1)}, u32[]{:S(2)}, u32[]{:S(2)}) %collective-permute-start.2) | collective-permute-done | bytes 524320 | tf_op jit(solution)/shard_map/ppermute | solution.py:19
  573.7 1.1 constant_dynamic-update-slice_fusion
  574.7 1.3 copy-done.3
  576.1 0.0 all-gather.18.cloned.1.call-update
  576.1 0.0 reduce-scatter.5.cloned.1.call-start
  576.1 0.0 copy-done.8
  576.2 12.2 %all-gather.2 = bf16[4096]{0:T(1024)(128)(2,1)S(1)} all-gather(bf16[1024]{0:T(1024)(128)(2,1)S(1)} %copy-done.8), channel_id=4, replica_groups=mesh['ba'=4,'ma'=4,'row'=2] {'ma'}, dimensions={0}, use_global_device_ids=true | all-gather | bytes 10240 | tf_op jit(solution)/shard_map/all_gather | solution.py:46
  588.3 42.8 %all-gather.18.cloned.1.call-done = bf16[512,4096]{1,0:T(8,128)(2,1)} async-done(((bf16[256,4096]{1,0:T(8,128)(2,1)}), bf16[512,4096]{1,0:T(8,128)(2,1)}) %all-gather.18.cloned.1.call-update) | async-done | bytes 4194320 | tf_op jit(solution)/shard_map/all_gather | solution.py:48
  631.1 3.2 fusion.1
  634.4 0.2 copy-done.4
  634.6 7.7 %fusion.28 = f32[512,1024]{1,0:T(8,128)S(1)} fusion(bf16[4096,1024]{1,0:T(8,128)(2,1)} %param.19, bf16[512,4096]{1,0:T(8,128)(2,1)S(1)} %copy-done.4, f32[4096]{0:T(1024)S(1)} %mul.113, f32[512]{0:T(512)S(1)} %add_rsqrt_fusion), kind=kOutput, calls=%fused_computation.38 | convolution fusion | flops 4303355904 | bytes 14698496 | tf_op jit(solution)/shard_map/dot_general | solution.py:121
  642.3 0.0 slice-done
  642.3 0.0 slice-done.1
  642.4 4.9 fusion.25
  647.3 0.0 copy-start.1
  647.3 6.2 fusion.12
  653.4 0.0 reduce-scatter.5.cloned.1.call-update
  653.5 88.5 %reduce-scatter.5.cloned.1.call-done = bf16[256,1024]{1,0:T(8,128)(2,1)} async-done(((bf16[2048,1024]{1,0:T(8,128)(2,1)}), bf16[256,1024]{1,0:T(8,128)(2,1)}) %reduce-scatter.5.cloned.1.call-update) | async-done | bytes 524304 | tf_op jit(solution)/shard_map/reduce_scatter | solution.py:127
  742.0 2.0 fusion.31
  744.0 0.0 copy-done.1
  (24 shorter events, 0.1 us)
Async XLA Ops:
  6.5 17.5 %copy-start = (f32[32,16]{0,1:T(8,128)S(1)}, f32[32,16]{0,1:T(8,128)}, u32[]{:S(2)}) copy-start(f32[32,16]{0,1:T(8,128)} %param.17) | copy-start | bytes 6148
  6.5 50.8 %all-gather.20.cloned.1.call-start = ((), (), s32[]{:S(2)}) async-start(), calls=%async_computation.9 | async-start | bytes 2621440 | tf_op jit(solution)/shard_map/all_gather | solution.py:79
  7.3 154.4 %all-gather.12.cloned.1.call-start = ((), (), s32[]{:S(2)}) async-start(), calls=%async_computation.3 | async-start | bytes 12582912 | tf_op jit(solution)/shard_map/all_gather | solution.py:74
  8.0 259.3 %all-gather.14.cloned.1.call-start = ((), (), s32[]{:S(2)}) async-start(), calls=%async_computation.4 | async-start | bytes 12582912 | tf_op jit(solution)/shard_map/all_gather | solution.py:75
  8.7 1.2 copy-start.7
  8.8 363.9 %all-gather.10.cloned.1.call-start = ((), (), s32[]{:S(2)}) async-start(), calls=%async_computation.2 | async-start | bytes 12582912 | tf_op jit(solution)/shard_map/all_gather | solution.py:76
  9.3 468.8 %all-gather.16.cloned.1.call-start = ((), (), s32[]{:S(2)}) async-start(), calls=%async_computation.5 | async-start | bytes 12582912 | tf_op jit(solution)/shard_map/all_gather | solution.py:109
  9.9 519.2 %reduce-scatter.3.cloned.1.call-start = ((), (), s32[]{:S(2)}) async-start(), calls=%async_computation.6 | async-start | bytes 2621440 | tf_op jit(solution)/shard_map/reduce_scatter | solution.py:112
  59.4 207.9 %copy-start.6 = (bf16[1,256,4096]{2,1,0:T(8,128)(2,1)S(1)}, bf16[1,256,4096]{2,1,0:T(8,128)(2,1)}, u32[]{:S(2)}) copy-start(bf16[1,256,4096]{2,1,0:T(8,128)(2,1)} %all-gather.20.cloned.1.call-done) | copy-start | bytes 6291460
  384.3 2.1 copy-start.2
  485.3 44.1 %copy-start.5 = (bf16[1,256,1024]{2,1,0:T(8,128)(2,1)S(1)}, bf16[1,256,1024]{2,1,0:T(8,128)(2,1)}, u32[]{:S(2)}) copy-start(bf16[1,256,1024]{2,1,0:T(8,128)(2,1)} %param.11) | copy-start | bytes 1572868
  485.3 145.8 %all-gather.18.cloned.1.call-start = ((), (), s32[]{:S(2)}) async-start(), calls=%async_computation.7 | async-start | bytes 6291456 | tf_op jit(solution)/shard_map/all_gather | solution.py:48
  529.3 46.8 %copy-start.8 = (bf16[1024]{0:T(1024)(128)(2,1)S(1)}, bf16[1024]{0:T(1024)(128)(2,1)}, u32[]{:S(2)}) copy-start(bf16[1024]{0:T(1024)(128)(2,1)} %param.18) | copy-start | bytes 6148
  530.6 15.1 %collective-permute-start = (bf16[256,1024]{1,0:T(8,128)(2,1)S(1)}, bf16[256,1024]{1,0:T(8,128)(2,1)S(1)}, u32[]{:S(2)}, u32[]{:S(2)}) collective-permute-start(bf16[256,1024]{1,0:T(8,128)(2,1)S(1)} %get-tuple-element.6), channel_id=1, source_target_pairs={{0,2},{2,4},{4,6},{6,0},{1,3},{3,5},{5,7},{7,1},{8,10},{10,12},{12... | collective-permute-start | bytes 1572872 | tf_op jit(solution)/shard_map/ppermute | solution.py:19
  545.7 14.3 %collective-permute-start.1 = (bf16[256,1024]{1,0:T(8,128)(2,1)S(1)}, bf16[256,1024]{1,0:T(8,128)(2,1)}, u32[]{:S(2)}, u32[]{:S(2)}) collective-permute-start(bf16[256,1024]{1,0:T(8,128)(2,1)S(1)} %collective-permute-done), channel_id=1, source_target_pairs={{0,2},{2,4},{4,6},{6,0},{1,3},{3,5},{5,7},{7,1},{8,10},{10,12},{12... | collective-permute-start | bytes 1572872 | tf_op jit(solution)/shard_map/ppermute | solution.py:19
  560.0 13.6 %collective-permute-start.2 = (bf16[256,1024]{1,0:T(8,128)(2,1)}, bf16[256,1024]{1,0:T(8,128)(2,1)}, u32[]{:S(2)}, u32[]{:S(2)}) collective-permute-start(bf16[256,1024]{1,0:T(8,128)(2,1)} %collective-permute-done.1), channel_id=1, source_target_pairs={{0,2},{2,4},{4,6},{6,0},{1,3},{3,5},{5,7},{7,1},{8,10},{10,12},{12... | collective-permute-start | bytes 1572872 | tf_op jit(solution)/shard_map/ppermute | solution.py:19
  574.7 1.3 copy-start.3
  576.1 165.9 %reduce-scatter.5.cloned.1.call-start = ((), (), s32[]{:S(2)}) async-start(), calls=%async_computation.8 | async-start | bytes 4718592 | tf_op jit(solution)/shard_map/reduce_scatter | solution.py:127
  631.1 3.4 copy-start.4
  631.1 11.2 %slice-start = ((s8[8388608]{0:T(1024)(128)(4,1)}), s8[4194304]{0:T(1024)(128)(4,1)S(1)}, s32[]{:S(2)}) async-start(s8[8388608]{0:T(1024)(128)(4,1)} %bitcast.55), calls=%async_computation.10 | async-start | bytes 8388608
  631.1 16.1 %slice-start.2 = ((s8[8388608]{0:T(1024)(128)(4,1)}), s8[4194304]{0:T(1024)(128)(4,1)S(1)}, s32[]{:S(2)}) async-start(s8[8388608]{0:T(1024)(128)(4,1)} %bitcast.57), calls=%async_computation.12 | async-start | bytes 8388608
  634.6 7.8 %slice-start.1 = ((s8[8388608]{0:T(1024)(128)(4,1)}), s8[4194304]{0:T(1024)(128)(4,1)S(1)}, s32[]{:S(2)}) async-start(s8[8388608]{0:T(1024)(128)(4,1)} %bitcast.55), calls=%async_computation.11 | async-start | bytes 8388608
  634.6 12.7 %slice-start.3 = ((s8[8388608]{0:T(1024)(128)(4,1)}), s8[4194304]{0:T(1024)(128)(4,1)S(1)}, s32[]{:S(2)}) async-start(s8[8388608]{0:T(1024)(128)(4,1)} %bitcast.57), calls=%async_computation.13 | async-start | bytes 8388608
  647.3 96.8 %copy-start.1 = (f32[32,16]{0,1:T(8,128)S(1)}, f32[32,16]{0,1:T(8,128)}, u32[]{:S(2)}) copy-start(f32[32,16]{0,1:T(8,128)} %param.17) | copy-start | bytes 6148
Sparse Core Ops, SparseCore 0:
  8.9 48.3 all-gather.19
  58.9 102.7 all-gather.11
  163.2 104.0 all-gather.13
  268.7 103.9 all-gather.9
  374.1 103.9 all-gather.15
  485.4 43.6 reduce-scatter.2
  576.2 54.8 all-gather.17
  653.6 88.3 reduce-scatter.4
